TPU v7x, 512 devices: a whole 4x4x16 slice. The times are simulated.
512 devices in a mesh: dp: 64 (over z, x), head: 8 (over y, core).
Axes of the slice: x: 4, y: 4, z: 16, core: 2. Of those that a mesh axis runs over, the one named last changes fastest.
Arguments:
- queries: bfloat16 [16384, 8192], P('dp', 'head'), may hold values from -6 to 6
- keys: bfloat16 [16384, 1024], P('dp', 'head'), may hold values from -6 to 6
- values: bfloat16 [16384, 1024], P('dp', 'head'), may hold values from -6 to 6
- output_grad: bfloat16 [16384, 4096], P('dp', 'head'), may hold values from -6 to 6
- out_weight: bfloat16 [8192, 4096], P(('head', 'dp')), may hold values from -0.0625 to 0.0625
- lengths: int32 [64], replicated, may hold values from 1 to 512, 16384 in all
Outputs:
- layer_out: bfloat16 [16384, 4096], P('dp', 'head')
- query_grad: bfloat16 [16384, 8192], P('dp', 'head')
- key_grad: bfloat16 [16384, 1024], P('dp', 'head')
- value_grad: bfloat16 [16384, 1024], P('dp', 'head')
Inputs may be any that keep to these rules, and one draw needn't show every extreme that they name: Each of the 64 lengths is at least 1 and at most 512, they sum to 16384, and one equals 512.
All inputs are finite; a program needn't handle non-finite values.
Results may differ from a plain program's by a relative error of at most 0.028.
Values may be sent and summed in bfloat16 or wider, within the bound.
No kernel may reach another device: no remote copies, remote signals or barrier semaphores. Data moves between devices by JAX's collectives and lax.ppermute only.
A program may use at most 128 MiB of HBM per device.

v0:
```python
import math
import jax
import jax.numpy as jnp
from jax import lax
from jax.sharding import Mesh
from jax.sharding import PartitionSpec as P

HD = 128
SPAN = 2
DP = ("dp_0", "dp_1")
HEAD_DP = ("head", "dp_0", "dp_1")
masked_score = -1e30


def gather_axes(x, axes, dim):
    filled = x
    for number in range(len(axes) - 1, -1, -1):
        filled = lax.all_gather(filled, axes[number], axis=dim, tiled=True)
    return filled


def in_order(pieces, dim):
    pieces = jnp.moveaxis(pieces, 0, dim)
    shape = pieces.shape
    return pieces.reshape(*shape[:dim], shape[dim] * shape[dim + 1], *shape[dim + 2 :])


def from_everyone(x, axis):
    size = lax.axis_size(axis)
    return lax.all_to_all(jnp.broadcast_to(x[None], (size, *x.shape)), axis, 0, 0, tiled=True)


def gather_directly(x, axis, dim):
    return in_order(from_everyone(x, axis), dim)


def passed_along(block, axis, distance):
    devices = range(lax.axis_size(axis))
    route = [(i - distance, i) for i in devices if i - distance in devices]
    return lax.ppermute(block, axis, route)


def in_blocks(x, dim, size):
    before, after = (x.shape[:dim], x.shape[dim + 1 :])
    return jnp.moveaxis(x.reshape(*before, size, -1, *after), dim, 0)


def sent_and_summed(x, axis, dim):
    pieces = in_blocks(x, dim, lax.axis_size(axis))
    arrived = lax.all_to_all(pieces, axis, split_axis=0, concat_axis=0, tiled=True)
    return arrived.astype(jnp.float32).sum(axis=0)


def doc_start(lengths, positions):
    doc_ends = jnp.cumsum(lengths)
    closed = doc_ends[None, :] <= positions[:, None]
    return jnp.sum(jnp.where(closed, lengths[None, :], 0), axis=1)


def attend(queries, key_rows, value_rows, d_attended, visible, head_dim):
    row_count = queries.shape[0]
    kv_heads = key_rows.shape[1] // head_dim
    group_ratio = queries.shape[1] // key_rows.shape[1]
    scaling = 1.0 / math.sqrt(head_dim)
    grouped = queries.reshape(row_count, kv_heads, group_ratio, head_dim)
    keyed = key_rows.reshape(-1, kv_heads, head_dim)
    valued = value_rows.reshape(-1, kv_heads, head_dim)
    upstream = d_attended.reshape(row_count, kv_heads, group_ratio, head_dim)
    scores = (
        jnp.einsum("tgrd,ngd->grtn", grouped, keyed, preferred_element_type=jnp.float32) * scaling
    )
    scores = jnp.where(visible[None, None], scores, masked_score)
    maximum = jnp.max(scores, axis=-1, keepdims=True)
    weights = jnp.exp(scores - maximum)
    shares = weights / jnp.sum(weights, axis=-1, keepdims=True)
    shares_low = shares.astype(jnp.bfloat16)
    attended = jnp.einsum(
        "grtn,ngd->tgrd", shares_low, valued, preferred_element_type=jnp.float32
    ).astype(jnp.bfloat16)
    row_dots = jnp.sum(upstream.astype(jnp.float32) * attended.astype(jnp.float32), axis=-1)
    d_shares = jnp.einsum("tgrd,ngd->grtn", upstream, valued, preferred_element_type=jnp.float32)
    dscore = (shares * (d_shares - jnp.transpose(row_dots, (1, 2, 0))[..., None]) * scaling).astype(
        jnp.bfloat16
    )
    query_grad = jnp.einsum(
        "grtn,ngd->tgrd", dscore, keyed, preferred_element_type=jnp.float32
    ).astype(jnp.bfloat16)
    key_part = jnp.einsum("grtn,tgrd->ngd", dscore, grouped, preferred_element_type=jnp.float32)
    value_part = jnp.einsum(
        "grtn,tgrd->ngd", shares_low, upstream, preferred_element_type=jnp.float32
    )
    return (
        attended.reshape(row_count, -1),
        query_grad.reshape(row_count, -1),
        key_part.reshape(-1, kv_heads * head_dim),
        value_part.reshape(-1, kv_heads * head_dim),
    )


def on_device(queries, keys, values, output_grad, out_weight, lengths):
    block_rows = queries.shape[0]
    device = lax.axis_index(DP)
    group_weight = lax.all_gather(out_weight, DP, axis=0, tiled=True)
    upstream_all = gather_directly(output_grad, "head", 1)
    d_attended = jnp.einsum(
        "tc,rc->tr", upstream_all, group_weight, preferred_element_type=jnp.float32
    ).astype(jnp.bfloat16)
    earlier = [passed_along((keys, values), DP, offset) for offset in range(1, SPAN + 1)]
    key_rows = jnp.concatenate([couple[0] for couple in earlier[::-1]] + [keys], axis=0)
    value_rows = jnp.concatenate([couple[1] for couple in earlier[::-1]] + [values], axis=0)
    owner_positions = device * block_rows + jnp.arange(block_rows, dtype=jnp.int32)
    owner_starts = doc_start(lengths, owner_positions)
    key_positions = (device - SPAN) * block_rows + jnp.arange(
        (SPAN + 1) * block_rows, dtype=jnp.int32
    )
    visible = (key_positions[None, :] >= owner_starts[:, None]) & (
        key_positions[None, :] <= owner_positions[:, None]
    )
    first_row = 0 * block_rows
    attended, query_grad, key_part, value_part = attend(
        queries, key_rows, value_rows, d_attended, visible, HD
    )
    padding = jnp.zeros((first_row, key_part.shape[1]), jnp.float32)
    attended, query_grad, key_all, value_all = (
        attended,
        query_grad,
        jnp.concatenate([padding, key_part], axis=0),
        jnp.concatenate([padding, value_part], axis=0),
    )
    projected = jnp.dot(attended, group_weight, preferred_element_type=jnp.float32)
    layer_out = sent_and_summed(projected.astype(jnp.bfloat16), "head", 1).astype(jnp.bfloat16)

    def block_of(all_rows, offset):
        return all_rows[(SPAN - offset) * block_rows : (SPAN - offset + 1) * block_rows]

    key_home = block_of(key_all, 0)
    value_home = block_of(value_all, 0)
    for offset in range(1, SPAN + 1):
        returned = (
            passed_along(block_of(key_all, offset).astype(jnp.bfloat16), DP, -offset).astype(
                jnp.float32
            ),
            passed_along(block_of(value_all, offset).astype(jnp.bfloat16), DP, -offset).astype(
                jnp.float32
            ),
        )
        key_home = key_home + returned[0]
        value_home = value_home + returned[1]
    return (layer_out, query_grad, key_home.astype(jnp.bfloat16), value_home.astype(jnp.bfloat16))


def solution(mesh):
    finer = Mesh(mesh.devices.reshape(16, 4, mesh.shape["head"]), ("dp_0", "dp_1", "head"))
    placed = (P(DP, "head"), P(DP, "head"), P(DP, "head"), P(DP, "head"), P(HEAD_DP, None), P())
    return jax.shard_map(
        on_device,
        mesh=finer,
        in_specs=placed,
        out_specs=(P(DP, "head"), P(DP, "head"), P(DP, "head"), P(DP, "head")),
        check_vma=False,
    )
```

profile of v0, /device:TPU:46, one launch (start us, length us, event | category | flops | bytes accessed | tf_op | source)
XLA Modules:
  0.0 230.2 jit_solution(14787751482215236873)
XLA Ops:
  7.2 0.0 copy-start
  7.2 0.0 copy-start.2
  7.2 0.0 copy-start.5
  7.2 0.0 all-gather.2.cloned.1.call-start
  7.2 0.7 all-gather.2.cloned.1.call-update
  7.9 3.7 %collective-permute-start.3 = (bf16[256,128]{1,0:T(8,128)(2,1)}, bf16[256,128]{1,0:T(8,128)(2,1)S(1)}, u32[]{:S(2)}, u32[]{:S(2)}) collective-permute-start(bf16[256,128]{1,0:T(8,128)(2,1)} %param.7), channel_id=1, source_target_pairs={{0,8},{8,16},{16,24},{24,32},{32,40},{40,48},{48,56},{56,64},{64,7... | collective-permute-start | bytes 196616 | tf_op jit(solution)/shard_map/ppermute | solution.py:40
  11.7 4.3 %collective-permute-start.2 = (bf16[256,128]{1,0:T(8,128)(2,1)}, bf16[256,128]{1,0:T(8,128)(2,1)S(1)}, u32[]{:S(2)}, u32[]{:S(2)}) collective-permute-start(bf16[256,128]{1,0:T(8,128)(2,1)} %param.7), channel_id=1, source_target_pairs={{0,16},{8,24},{16,32},{24,40},{32,48},{40,56},{48,64},{56,72},{64,... | collective-permute-start | bytes 196616 | tf_op jit(solution)/shard_map/ppermute | solution.py:40
  16.0 0.9 copy.60
  17.0 3.7 %collective-permute-start.1 = (bf16[256,128]{0,1:T(8,128)(2,1)S(1)}, bf16[256,128]{0,1:T(8,128)(2,1)}, u32[]{:S(2)}, u32[]{:S(2)}) collective-permute-start(bf16[256,128]{0,1:T(8,128)(2,1)S(1)} %copy.60), channel_id=1, source_target_pairs={{0,8},{8,16},{16,24},{24,32},{32,40},{40,48},{48,56},{56,64},{64,7... | collective-permute-start | bytes 196616 | tf_op jit(solution)/shard_map/ppermute | solution.py:40
  20.7 3.5 %collective-permute-start = (bf16[256,128]{0,1:T(8,128)(2,1)S(1)}, bf16[256,128]{0,1:T(8,128)(2,1)}, u32[]{:S(2)}, u32[]{:S(2)}) collective-permute-start(bf16[256,128]{0,1:T(8,128)(2,1)S(1)} %copy.60), channel_id=1, source_target_pairs={{0,16},{8,24},{16,32},{24,40},{32,48},{40,56},{48,64},{56,72},{64,... | collective-permute-start | bytes 196616 | tf_op jit(solution)/shard_map/ppermute | solution.py:40
  24.1 1.1 copy.67
  25.2 1.4 broadcast_in_dim.30
  26.7 4.9 %all-to-all-start.1 = ((bf16[8,256,512]{1,2,0:T(8,128)(2,1)}), bf16[8,256,512]{1,2,0:T(8,128)(2,1)S(1)}, u32[]{:S(2)}, u32[]{:S(2)}) async-start(bf16[8,256,512]{1,2,0:T(8,128)(2,1)} %broadcast_in_dim.30), calls=%async_computation.1 | async-start | bytes 4194304 | tf_op jit(solution)/shard_map/all_to_all | solution.py:30
  31.6 0.0 copy-done.5
  31.6 0.1 copy.63
  31.7 0.1 reduce-window.8
  31.8 0.1 reduce.4
  31.9 0.1 select_reduce_fusion
  32.0 0.2 compare_and_fusion
  32.3 0.0 collective-permute-done.3
  32.3 0.0 collective-permute-done.2
  32.3 0.0 copy-done
  32.3 0.0 copy-done.2
  32.3 0.0 copy-start.3
  32.3 1.1 fusion.5
  33.4 0.0 copy-start.1
  33.5 1.3 fusion.4
  34.8 0.0 copy-done.3
  34.8 1.4 copy-done.1
  36.1 3.1 %convert_bitcast_fusion = bf16[8,256,768]{1,2,0:T(8,128)(2,1)} fusion(f32[8,256]{1,0:T(8,128)S(1)} %fusion.4, f32[8,256]{1,0:T(8,128)S(1)} %get-tuple-element.24, f32[768,256,8]{1,0,2:T(8,128)S(1)} %get-tuple-element.25, pred[256,768]{0,1:T(8,128)(4,1)S(1)} %compare_and_fusion), kind=kLoop, calls=%fused_computation.11 | loop fusion | flops 7864320 | bytes 9650176 | tf_op jit(solution)/shard_map/reshape.20
  39.2 5.1 %copy.74 = bf16[8,256,768]{2,0,1:T(8,128)(2,1)} copy(bf16[8,256,768]{1,2,0:T(8,128)(2,1)} %convert_bitcast_fusion) | data formatting | bytes 6291456 | tf_op jit(solution)/shard_map/reshape.20
  44.3 13.0 %all-to-all-done.1 = bf16[8,256,512]{1,2,0:T(8,128)(2,1)S(1)} async-done(((bf16[8,256,512]{1,2,0:T(8,128)(2,1)}), bf16[8,256,512]{1,2,0:T(8,128)(2,1)S(1)}, u32[]{:S(2)}, u32[]{:S(2)}) %all-to-all-start.1) | async-done | bytes 2097184 | tf_op jit(solution)/shard_map/all_to_all | solution.py:30
  57.3 111.5 %all-gather.2.cloned.1.call-done = bf16[1024,4096]{1,0:T(8,128)(2,1)} async-done(((bf16[16,4096]{1,0:T(8,128)(2,1)}), bf16[1024,4096]{1,0:T(8,128)(2,1)}) %all-gather.2.cloned.1.call-update) | async-done | bytes 8388624 | tf_op jit(solution)/shard_map/all_gather | solution.py:103
  168.9 5.8 %convolution_convert_fusion.1 = bf16[256,1024]{1,0:T(8,128)(2,1)S(1)} fusion(bf16[256,4096]{0,1:T(8,128)(2,1)S(1)} %bitcast.148, bf16[1024,4096]{1,0:T(8,128)(2,1)} %all-gather.2.cloned.1.call-done), kind=kOutput, calls=%fused_computation.13 | convolution fusion | flops 2147745792 | bytes 11010048 | tf_op jit(solution)/shard_map/tc,rc->tr/dot_general | solution.py:105
  174.6 0.2 copy.70
  174.8 0.0 collective-permute-done.1
  174.8 0.0 collective-permute-done
  174.9 3.2 %multiply_reduce_fusion = (f32[256,8]{0,1:T(8,128)}, bf16[128,8,256]{2,0,1:T(8,128)(2,1)S(1)}) fusion(f32[256,1,8,128]{0,3,2,1:T(8,128)S(1)} %bitcast.145, bf16[8,256,768]{1,2,0:T(8,128)(2,1)} %convert_bitcast_fusion, bf16[256,128]{0,1:T(8,128)(2,1)S(1)} %copy.60, bf16[256,128]{0,1:T(8,128)(2,1)} %collective-permute-done.1, ...), kind=kOutput, calls=%fused_computation.18 | convolution fusion | flops 404289536 | bytes 4923392 | tf_op jit(solution)/shard_map/grtn,ngd->tgrd/dot_general | solution.py:77
  178.0 5.8 %convolution_convert_fusion = bf16[256,4096]{1,0:T(8,128)(2,1)S(1)} fusion(bf16[256,1024]{0,1:T(8,128)(2,1)S(1)} %bitcast.146, bf16[1024,4096]{1,0:T(8,128)(2,1)} %all-gather.2.cloned.1.call-done), kind=kOutput, calls=%fused_computation.8 | convolution fusion | flops 2148532224 | bytes 11010048 | tf_op jit(solution)/shard_map/dot_general | solution.py:130
  183.8 1.6 copy.104
  185.3 5.0 %all-to-all-start = ((bf16[8,256,512]{2,1,0:T(8,128)(2,1)}), bf16[8,256,512]{2,1,0:T(8,128)(2,1)S(1)}, u32[]{:S(2)}, u32[]{:S(2)}) async-start(bf16[8,256,512]{2,1,0:T(8,128)(2,1)} %bitcast.144), calls=%async_computation | async-start | bytes 4194304 | tf_op jit(solution)/shard_map/all_to_all | solution.py:50
  190.4 0.1 copy.86
  190.5 3.3 %fusion.25 = (bf16[768,1,128]{0,2,1:T(8,128)(2,1)S(1)}, f32[768,1,128]{0,2,1:T(8,128)}) fusion(bf16[256,8,128]{2,1,0:T(8,128)(2,1)S(1)} %bitcast.150, bf16[8,256,768]{2,0,1:T(8,128)(2,1)} %copy.74), kind=kOutput, calls=%fused_computation.49 | convolution fusion | flops 402751488 | bytes 4259840 | tf_op jit(solution)/shard_map/grtn,tgrd->ngd/dot_general | solution.py:89
  193.8 0.7 slice_bitcast_fusion.3
  194.4 3.7 %collective-permute-start.7 = (bf16[256,128]{0,1:T(8,128)(2,1)}, bf16[256,128]{0,1:T(8,128)(2,1)}, u32[]{:S(2)}, u32[]{:S(2)}) collective-permute-start(bf16[256,128]{0,1:T(8,128)(2,1)} %get-tuple-element.21), channel_id=1, source_target_pairs={{16,0},{24,8},{32,16},{40,24},{48,32},{56,40},{64,48},{72,56},{80,... | collective-permute-start | bytes 196616 | tf_op jit(solution)/shard_map/ppermute | solution.py:40
  198.2 3.3 %collective-permute-start.6 = (bf16[256,128]{0,1:T(8,128)(2,1)}, bf16[256,128]{0,1:T(8,128)(2,1)}, u32[]{:S(2)}, u32[]{:S(2)}) collective-permute-start(bf16[256,128]{0,1:T(8,128)(2,1)} %get-tuple-element.20), channel_id=1, source_target_pairs={{8,0},{16,8},{24,16},{32,24},{40,32},{48,40},{56,48},{64,56},{72,6... | collective-permute-start | bytes 196616 | tf_op jit(solution)/shard_map/ppermute | solution.py:40
  201.5 0.0 copy-start.4
  201.5 4.5 %fusion.6 = bf16[8,256,768]{1,2,0:T(8,128)(2,1)S(1)} fusion(f32[8,256]{1,0:T(8,128)} %bitcast.151, f32[8,256]{1,0:T(8,128)S(1)} %fusion.4, f32[8,256]{1,0:T(8,128)S(1)} %get-tuple-element.24, f32[768,256,8]{1,0,2:T(8,128)} %copy-done.1, pred[256,768]{0,1:T(8,128)(4,1)S(1)} %compare_and_fusion, bf16[256,128]{0,1:T(8,128)(2,1)S(1)} %copy.60, ...), kind=kOutput, calls=%fused_computation.10 | convolution fusion | flops 415825920 | bytes 10379264 | tf_op jit(solution)/shard_map/tgrd,ngd->grtn/dot_general | solution.py:81
  206.0 0.0 copy-done.4
  206.0 0.6 convolution_convert_fusion.2
  206.6 1.0 fusion.24
  207.6 0.7 slice_bitcast_fusion.5
  208.3 1.0 copy.75
  209.3 3.9 %collective-permute-start.5 = (bf16[256,128]{1,0:T(8,128)(2,1)}, bf16[256,128]{1,0:T(8,128)(2,1)S(1)}, u32[]{:S(2)}, u32[]{:S(2)}) collective-permute-start(bf16[256,128]{1,0:T(8,128)(2,1)} %get-tuple-element.23), channel_id=1, source_target_pairs={{16,0},{24,8},{32,16},{40,24},{48,32},{56,40},{64,48},{72,56},{80,... | collective-permute-start | bytes 196616 | tf_op jit(solution)/shard_map/ppermute | solution.py:40
  213.2 2.7 %collective-permute-start.4 = (bf16[256,128]{1,0:T(8,128)(2,1)}, bf16[256,128]{1,0:T(8,128)(2,1)S(1)}, u32[]{:S(2)}, u32[]{:S(2)}) collective-permute-start(bf16[256,128]{1,0:T(8,128)(2,1)} %get-tuple-element.22), channel_id=1, source_target_pairs={{8,0},{16,8},{24,16},{32,24},{40,32},{48,40},{56,48},{64,56},{72,6... | collective-permute-start | bytes 196616 | tf_op jit(solution)/shard_map/ppermute | solution.py:40
  215.9 0.0 collective-permute-done.7
  215.9 0.0 collective-permute-done.6
  216.0 1.0 fusion.16
  216.9 0.7 copy.76
  217.7 0.4 collective-permute-done.5
  218.1 3.6 %collective-permute-done.4 = bf16[256,128]{1,0:T(8,128)(2,1)S(1)} collective-permute-done((bf16[256,128]{1,0:T(8,128)(2,1)}, bf16[256,128]{1,0:T(8,128)(2,1)S(1)}, u32[]{:S(2)}, u32[]{:S(2)}) %collective-permute-start.4) | collective-permute-done | bytes 65568 | tf_op jit(solution)/shard_map/ppermute | solution.py:40
  221.7 0.7 fusion.19
  222.3 0.0 all-to-all-done
  222.3 1.0 reduce_sum.43
  (2 shorter events, 0.0 us)
Async XLA Ops:
  7.2 25.1 %copy-start = (bf16[256,1024]{1,0:T(8,128)(2,1)S(1)}, bf16[256,1024]{1,0:T(8,128)(2,1)}, u32[]{:S(2)}) copy-start(bf16[256,1024]{1,0:T(8,128)(2,1)} %param.6) | copy-start | bytes 1572868
  7.2 25.1 %copy-start.2 = (bf16[256,128]{1,0:T(8,128)(2,1)S(1)}, bf16[256,128]{1,0:T(8,128)(2,1)}, u32[]{:S(2)}) copy-start(bf16[256,128]{1,0:T(8,128)(2,1)} %param.7) | copy-start | bytes 196612
  7.2 24.4 %copy-start.5 = (s32[64]{0:T(128)S(1)}, s32[64]{0:T(128)}, u32[]{:S(2)}) copy-start(s32[64]{0:T(128)} %param.11) | copy-start | bytes 772
  7.2 161.7 %all-gather.2.cloned.1.call-start = ((), (), s32[]{:S(2)}) async-start(), calls=%async_computation.2 | async-start | bytes 8519680 | tf_op jit(solution)/shard_map/all_gather | solution.py:103
  7.9 24.3 %collective-permute-start.3 = (bf16[256,128]{1,0:T(8,128)(2,1)}, bf16[256,128]{1,0:T(8,128)(2,1)S(1)}, u32[]{:S(2)}, u32[]{:S(2)}) collective-permute-start(bf16[256,128]{1,0:T(8,128)(2,1)} %param.7), channel_id=1, source_target_pairs={{0,8},{8,16},{16,24},{24,32},{32,40},{40,48},{48,56},{56,64},{64,7... | collective-permute-start | bytes 196616 | tf_op jit(solution)/shard_map/ppermute | solution.py:40
  11.7 20.6 %collective-permute-start.2 = (bf16[256,128]{1,0:T(8,128)(2,1)}, bf16[256,128]{1,0:T(8,128)(2,1)S(1)}, u32[]{:S(2)}, u32[]{:S(2)}) collective-permute-start(bf16[256,128]{1,0:T(8,128)(2,1)} %param.7), channel_id=1, source_target_pairs={{0,16},{8,24},{16,32},{24,40},{32,48},{40,56},{48,64},{56,72},{64,... | collective-permute-start | bytes 196616 | tf_op jit(solution)/shard_map/ppermute | solution.py:40
  17.0 157.9 %collective-permute-start.1 = (bf16[256,128]{0,1:T(8,128)(2,1)S(1)}, bf16[256,128]{0,1:T(8,128)(2,1)}, u32[]{:S(2)}, u32[]{:S(2)}) collective-permute-start(bf16[256,128]{0,1:T(8,128)(2,1)S(1)} %copy.60), channel_id=1, source_target_pairs={{0,8},{8,16},{16,24},{24,32},{32,40},{40,48},{48,56},{56,64},{64,7... | collective-permute-start | bytes 196616 | tf_op jit(solution)/shard_map/ppermute | solution.py:40
  20.7 154.2 %collective-permute-start = (bf16[256,128]{0,1:T(8,128)(2,1)S(1)}, bf16[256,128]{0,1:T(8,128)(2,1)}, u32[]{:S(2)}, u32[]{:S(2)}) collective-permute-start(bf16[256,128]{0,1:T(8,128)(2,1)S(1)} %copy.60), channel_id=1, source_target_pairs={{0,16},{8,24},{16,32},{24,40},{32,48},{40,56},{48,64},{56,72},{64,... | collective-permute-start | bytes 196616 | tf_op jit(solution)/shard_map/ppermute | solution.py:40
  26.7 30.6 %all-to-all-start.1 = ((bf16[8,256,512]{1,2,0:T(8,128)(2,1)}), bf16[8,256,512]{1,2,0:T(8,128)(2,1)S(1)}, u32[]{:S(2)}, u32[]{:S(2)}) async-start(bf16[8,256,512]{1,2,0:T(8,128)(2,1)} %broadcast_in_dim.30), calls=%async_computation.1 | async-start | bytes 4194304 | tf_op jit(solution)/shard_map/all_to_all | solution.py:30
  32.3 2.5 %copy-start.3 = (bf16[256,128]{1,0:T(8,128)(2,1)}, bf16[256,128]{1,0:T(8,128)(2,1)S(1)}, u32[]{:S(2)}) copy-start(bf16[256,128]{1,0:T(8,128)(2,1)S(1)} %collective-permute-done.2) | copy-start | bytes 196612
  33.4 2.7 %copy-start.1 = (f32[768,256,8]{1,0,2:T(8,128)}, f32[768,256,8]{1,0,2:T(8,128)S(1)}, u32[]{:S(2)}) copy-start(f32[768,256,8]{1,0,2:T(8,128)S(1)} %get-tuple-element.25) | copy-start | bytes 18874372
  185.3 37.0 %all-to-all-start = ((bf16[8,256,512]{2,1,0:T(8,128)(2,1)}), bf16[8,256,512]{2,1,0:T(8,128)(2,1)S(1)}, u32[]{:S(2)}, u32[]{:S(2)}) async-start(bf16[8,256,512]{2,1,0:T(8,128)(2,1)} %bitcast.144), calls=%async_computation | async-start | bytes 4194304 | tf_op jit(solution)/shard_map/all_to_all | solution.py:50
  194.4 21.5 %collective-permute-start.7 = (bf16[256,128]{0,1:T(8,128)(2,1)}, bf16[256,128]{0,1:T(8,128)(2,1)}, u32[]{:S(2)}, u32[]{:S(2)}) collective-permute-start(bf16[256,128]{0,1:T(8,128)(2,1)} %get-tuple-element.21), channel_id=1, source_target_pairs={{16,0},{24,8},{32,16},{40,24},{48,32},{56,40},{64,48},{72,56},{80,... | collective-permute-start | bytes 196616 | tf_op jit(solution)/shard_map/ppermute | solution.py:40
  198.2 17.8 %collective-permute-start.6 = (bf16[256,128]{0,1:T(8,128)(2,1)}, bf16[256,128]{0,1:T(8,128)(2,1)}, u32[]{:S(2)}, u32[]{:S(2)}) collective-permute-start(bf16[256,128]{0,1:T(8,128)(2,1)} %get-tuple-element.20), channel_id=1, source_target_pairs={{8,0},{16,8},{24,16},{32,24},{40,32},{48,40},{56,48},{64,56},{72,6... | collective-permute-start | bytes 196616 | tf_op jit(solution)/shard_map/ppermute | solution.py:40
  201.5 4.5 %copy-start.4 = (bf16[256,128]{1,0:T(8,128)(2,1)S(1)}, bf16[256,128]{1,0:T(8,128)(2,1)}, u32[]{:S(2)}) copy-start(bf16[256,128]{1,0:T(8,128)(2,1)} %copy-done.3) | copy-start | bytes 196612
  209.3 8.8 %collective-permute-start.5 = (bf16[256,128]{1,0:T(8,128)(2,1)}, bf16[256,128]{1,0:T(8,128)(2,1)S(1)}, u32[]{:S(2)}, u32[]{:S(2)}) collective-permute-start(bf16[256,128]{1,0:T(8,128)(2,1)} %get-tuple-element.23), channel_id=1, source_target_pairs={{16,0},{24,8},{32,16},{40,24},{48,32},{56,40},{64,48},{72,56},{80,... | collective-permute-start | bytes 196616 | tf_op jit(solution)/shard_map/ppermute | solution.py:40
  213.2 8.5 %collective-permute-start.4 = (bf16[256,128]{1,0:T(8,128)(2,1)}, bf16[256,128]{1,0:T(8,128)(2,1)S(1)}, u32[]{:S(2)}, u32[]{:S(2)}) collective-permute-start(bf16[256,128]{1,0:T(8,128)(2,1)} %get-tuple-element.22), channel_id=1, source_target_pairs={{8,0},{16,8},{24,16},{32,24},{40,32},{48,40},{56,48},{64,56},{72,6... | collective-permute-start | bytes 196616 | tf_op jit(solution)/shard_map/ppermute | solution.py:40
Sparse Core Ops, SparseCore 0:
  11.0 157.8 all-gather.1
where the time goes:
time: 231 us; the launch traced here: 230 us
  waiting for transfers between devices  129 us (56%)
  starting transfers between devices  38.9 us (17%)
  matrix products  25.2 us (11%)
  local copies, waits for them, and re-layouts  15 us (6%)
  between operations  14.3 us (6%)
  other arithmetic  7.6 us (3%)
    all_gather x1, waiting for transfers between devices, on_device(): group_weight = lax.all_gather(out_weight, DP, axis=0, tiled=True)  112 us
    ppermute x8, starting transfers between devices, passed_along(): return lax.ppermute(block, axis, route)  28.9 us
    all_to_all x1, waiting for transfers between devices, from_everyone(): lax.all_to_all(jnp.broadcast_to(x[None], (size, *x.shape)), axis, 0, 0, t...  13 us
    dot_general x1, matrix products, on_device(): jnp.einsum('tc,rc->tr', upstream_all, group_weight, preferred_element_typ...  5.76 us
    dot_general x1, matrix products, on_device(): jnp.dot(attended, group_weight, preferred_element_type=jnp.float32)  5.75 us
    unnamed x17, local copies, waits for them, and re-layouts  5.25 us
    another operation x2, local copies, waits for them, and re-layouts  5.16 us
    all_to_all x1, starting transfers between devices, sent_and_summed(): lax.all_to_all(pieces, axis, split_axis=0, concat_axis=0, tiled=True)  5.02 us
  transfers between devices with their start and end apart: 11, of which 4 were waited for; matrix products, arithmetic and copies ran while one was open for 15% of the time, Pallas kernels for 0%

commit v1 on v0

--- a/solution.py
+++ b/solution.py
@@ -100,7 +100,10 @@
 def on_device(queries, keys, values, output_grad, out_weight, lengths):
     block_rows = queries.shape[0]
     device = lax.axis_index(DP)
-    group_weight = lax.all_gather(out_weight, DP, axis=0, tiled=True)
+    state_next = jax.lax.axis_size(DP)
+    latest = jnp.stack([out_weight] * state_next)
+    v_next = jax.lax.all_to_all(latest, DP, 0, 0)
+    group_weight = jnp.concatenate(v_next, axis=0)
     upstream_all = gather_directly(output_grad, "head", 1)
     d_attended = jnp.einsum(
         "tc,rc->tr", upstream_all, group_weight, preferred_element_type=jnp.float32

time: 231 us -> 484 us (2.10)
  the two profiles are of different devices: /device:TPU:46 before, /device:TPU:110 now
where the time goes in v1:
time: 484 us
  waiting for transfers between devices  349 us (72%)
  starting transfers between devices  53.3 us (11%)
  blocking collectives  30.7 us (6%)
  matrix products  25.1 us (5%)
  local copies, waits for them, and re-layouts  17.1 us (4%)
  other arithmetic  7.62 us (2%)
    ppermute x8, waiting for transfers between devices, passed_along(): return lax.ppermute(block, axis, route)  349 us
    ppermute x8, starting transfers between devices, passed_along(): return lax.ppermute(block, axis, route)  31 us
    all_to_all x1, blocking collectives, from_everyone(): lax.all_to_all(jnp.broadcast_to(x[None], (size, *x.shape)), axis, 0, 0, t...  30.7 us
    all_to_all x1, starting transfers between devices, on_device(): v_next = jax.lax.all_to_all(latest, DP, 0, 0)  17.5 us
  transfers between devices with their start and end apart: 10, of which 4 were waited for; matrix products, arithmetic and copies ran while one was open for 6% of the time, Pallas kernels for 0%

profile of v1, /device:TPU:110, one launch (start us, length us, event | category | flops | bytes accessed | tf_op | source)
XLA Modules:
  0.0 483.7 jit_solution(2114426781003863295)
XLA Ops:
  0.6 0.0 copy-start
  0.6 0.0 copy-start.2
  0.7 1.2 copy.67
  1.8 0.1 broadcast_in_dim.30
  2.0 30.7 %all_to_all.15 = bf16[8,256,512]{1,2,0:T(8,128)(2,1)S(1)} all-to-all(bf16[8,256,512]{1,2,0:T(8,128)(2,1)S(1)} %broadcast_in_dim.30), channel_id=1, replica_groups=mesh['dp_0'=16,'dp_1'=4,'head'=8] {'head'}, dimensions={0} | all-to-all | bytes 4194304 | tf_op jit(solution)/shard_map/all_to_all | solution.py:30
  32.7 0.0 copy-done.2
  32.7 4.3 stack.2
  36.9 0.0 copy-start.3
  36.9 17.5 %all-to-all-start = ((bf16[64,16,4096]{2,1,0:T(8,128)(2,1)}), bf16[64,16,4096]{2,1,0:T(8,128)(2,1)}, u32[]{:S(2)}, u32[]{:S(2)}) async-start(bf16[64,16,4096]{2,1,0:T(8,128)(2,1)} %stack.2), calls=%async_computation | async-start | bytes 16777216 | tf_op jit(solution)/shard_map/all_to_all | solution.py:105
  54.5 0.0 copy-done.3
  54.5 4.6 collective-permute-start.3
  59.1 4.3 collective-permute-start.2
  63.4 0.0 copy-done.6
  63.4 0.1 copy.60
  63.5 3.7 collective-permute-start.1
  67.2 3.3 collective-permute-start
  70.4 0.0 copy-done.7
  70.5 0.1 copy.63
  70.6 0.1 reduce-window.8
  70.7 0.1 reduce.4
  70.8 0.1 select_reduce_fusion
  70.9 0.2 compare_and_fusion
  71.1 341.7 %collective-permute-done.3 = bf16[256,128]{1,0:T(8,128)(2,1)S(1)} collective-permute-done((bf16[256,128]{1,0:T(8,128)(2,1)S(1)}, bf16[256,128]{1,0:T(8,128)(2,1)S(1)}, u32[]{:S(2)}, u32[]{:S(2)}) %collective-permute-start.3) | collective-permute-done | bytes 65568 | tf_op jit(solution)/shard_map/ppermute | solution.py:40
  412.9 2.5 collective-permute-done.2
  415.4 0.0 copy-done
  415.4 1.1 fusion.5
  416.5 0.0 copy-start.1
  416.5 1.3 fusion.4
  417.8 0.0 copy-done.4
  417.8 1.3 copy-done.1
  419.1 3.1 convert_bitcast_fusion
  422.3 5.1 %copy.74 = bf16[8,256,768]{2,0,1:T(8,128)(2,1)} copy(bf16[8,256,768]{1,2,0:T(8,128)(2,1)} %convert_bitcast_fusion) | data formatting | bytes 6291456 | tf_op jit(solution)/shard_map/reshape.10
  427.3 0.0 all-to-all-done
  427.3 5.8 %convolution_convert_fusion.1 = bf16[256,1024]{1,0:T(8,128)(2,1)S(1)} fusion(bf16[256,4096]{0,1:T(8,128)(2,1)S(1)} %bitcast.149, bf16[1024,4096]{1,0:T(8,128)(2,1)} %bitcast.9), kind=kOutput, calls=%fused_computation.13 | convolution fusion | flops 2147745792 | bytes 11010048 | tf_op jit(solution)/shard_map/tc,rc->tr/dot_general | solution.py:108
  433.1 0.2 copy.70
  433.3 0.0 collective-permute-done.1
  433.3 0.0 collective-permute-done
  433.3 3.2 multiply_reduce_fusion
  436.5 5.8 %convolution_convert_fusion = bf16[256,4096]{1,0:T(8,128)(2,1)S(1)} fusion(bf16[256,1024]{0,1:T(8,128)(2,1)S(1)} %bitcast.147, bf16[1024,4096]{1,0:T(8,128)(2,1)} %bitcast.9), kind=kOutput, calls=%fused_computation.8 | convolution fusion | flops 2148532224 | bytes 11010048 | tf_op jit(solution)/shard_map/dot_general | solution.py:133
  442.2 1.5 copy.104
  443.8 4.7 all-to-all-start.1
  448.5 0.1 copy.86
  448.6 3.3 fusion.25
  451.9 0.7 slice_bitcast_fusion.3
  452.6 7.7 %collective-permute-start.7 = (bf16[256,128]{0,1:T(8,128)(2,1)}, bf16[256,128]{0,1:T(8,128)(2,1)}, u32[]{:S(2)}, u32[]{:S(2)}) collective-permute-start(bf16[256,128]{0,1:T(8,128)(2,1)} %get-tuple-element.21), channel_id=1, source_target_pairs={{16,0},{24,8},{32,16},{40,24},{48,32},{56,40},{64,48},{72,56},{80,... | collective-permute-start | bytes 196616 | tf_op jit(solution)/shard_map/ppermute | solution.py:40
  460.3 2.1 collective-permute-start.6
  462.4 0.0 copy-start.5
  462.4 4.5 fusion.6
  466.9 0.0 copy-done.5
  466.9 0.6 convolution_convert_fusion.2
  467.5 1.0 fusion.24
  468.5 0.7 slice_bitcast_fusion.5
  469.2 1.0 copy.75
  470.2 2.1 collective-permute-start.5
  472.3 3.2 collective-permute-start.4
  475.5 0.0 collective-permute-done.7
  475.6 0.0 collective-permute-done.6
  475.6 1.0 fusion.16
  476.5 0.7 copy.76
  477.3 3.1 collective-permute-done.5
  480.4 1.7 collective-permute-done.4
  482.0 0.7 fusion.19
  482.7 0.0 all-to-all-done.1
  482.7 1.0 reduce_sum.43
  (5 shorter events, 0.0 us)
Async XLA Ops:
  0.6 414.8 %copy-start = (bf16[256,1024]{1,0:T(8,128)(2,1)S(1)}, bf16[256,1024]{1,0:T(8,128)(2,1)}, u32[]{:S(2)}) copy-start(bf16[256,1024]{1,0:T(8,128)(2,1)} %param.6) | copy-start | bytes 1572868
  0.6 32.0 %copy-start.2 = (bf16[16,4096]{1,0:T(8,128)(2,1)S(1)}, bf16[16,4096]{1,0:T(8,128)(2,1)}, u32[]{:S(2)}) copy-start(bf16[16,4096]{1,0:T(8,128)(2,1)} %param.10) | copy-start | bytes 393220
  36.9 17.6 %copy-start.3 = (bf16[256,128]{1,0:T(8,128)(2,1)S(1)}, bf16[256,128]{1,0:T(8,128)(2,1)}, u32[]{:S(2)}) copy-start(bf16[256,128]{1,0:T(8,128)(2,1)} %param.7) | copy-start | bytes 196612
  36.9 26.4 %copy-start.6 = (bf16[256,128]{1,0:T(8,128)(2,1)S(1)}, bf16[256,128]{1,0:T(8,128)(2,1)}, u32[]{:S(2)}) copy-start(bf16[256,128]{1,0:T(8,128)(2,1)} %param.8) | copy-start | bytes 196612
  36.9 33.5 %copy-start.7 = (s32[64]{0:T(128)S(1)}, s32[64]{0:T(128)}, u32[]{:S(2)}) copy-start(s32[64]{0:T(128)} %param.11) | copy-start | bytes 772
  36.9 390.4 %all-to-all-start = ((bf16[64,16,4096]{2,1,0:T(8,128)(2,1)}), bf16[64,16,4096]{2,1,0:T(8,128)(2,1)}, u32[]{:S(2)}, u32[]{:S(2)}) async-start(bf16[64,16,4096]{2,1,0:T(8,128)(2,1)} %stack.2), calls=%async_computation | async-start | bytes 16777216 | tf_op jit(solution)/shard_map/all_to_all | solution.py:105
  54.5 358.4 %collective-permute-start.3 = (bf16[256,128]{1,0:T(8,128)(2,1)S(1)}, bf16[256,128]{1,0:T(8,128)(2,1)S(1)}, u32[]{:S(2)}, u32[]{:S(2)}) collective-permute-start(bf16[256,128]{1,0:T(8,128)(2,1)S(1)} %copy-done.3), channel_id=1, source_target_pairs={{0,8},{8,16},{16,24},{24,32},{32,40},{40,48},{48,56},{56,64},{64,7... | collective-permute-start | bytes 196616 | tf_op jit(solution)/shard_map/ppermute | solution.py:40
  59.1 356.3 %collective-permute-start.2 = (bf16[256,128]{1,0:T(8,128)(2,1)S(1)}, bf16[256,128]{1,0:T(8,128)(2,1)S(1)}, u32[]{:S(2)}, u32[]{:S(2)}) collective-permute-start(bf16[256,128]{1,0:T(8,128)(2,1)S(1)} %copy-done.3), channel_id=1, source_target_pairs={{0,16},{8,24},{16,32},{24,40},{32,48},{40,56},{48,64},{56,72},{64,... | collective-permute-start | bytes 196616 | tf_op jit(solution)/shard_map/ppermute | solution.py:40
  63.5 369.8 %collective-permute-start.1 = (bf16[256,128]{0,1:T(8,128)(2,1)S(1)}, bf16[256,128]{0,1:T(8,128)(2,1)}, u32[]{:S(2)}, u32[]{:S(2)}) collective-permute-start(bf16[256,128]{0,1:T(8,128)(2,1)S(1)} %copy.60), channel_id=1, source_target_pairs={{0,8},{8,16},{16,24},{24,32},{32,40},{40,48},{48,56},{56,64},{64,7... | collective-permute-start | bytes 196616 | tf_op jit(solution)/shard_map/ppermute | solution.py:40
  67.2 366.1 %collective-permute-start = (bf16[256,128]{0,1:T(8,128)(2,1)S(1)}, bf16[256,128]{0,1:T(8,128)(2,1)}, u32[]{:S(2)}, u32[]{:S(2)}) collective-permute-start(bf16[256,128]{0,1:T(8,128)(2,1)S(1)} %copy.60), channel_id=1, source_target_pairs={{0,16},{8,24},{16,32},{24,40},{32,48},{40,56},{48,64},{56,72},{64,... | collective-permute-start | bytes 196616 | tf_op jit(solution)/shard_map/ppermute | solution.py:40
  415.4 2.4 copy-start.4
  416.5 2.6 copy-start.1
  443.8 38.9 %all-to-all-start.1 = ((bf16[8,256,512]{2,1,0:T(8,128)(2,1)}), bf16[8,256,512]{2,1,0:T(8,128)(2,1)S(1)}, u32[]{:S(2)}, u32[]{:S(2)}) async-start(bf16[8,256,512]{2,1,0:T(8,128)(2,1)} %bitcast.145), calls=%async_computation.1 | async-start | bytes 4194304 | tf_op jit(solution)/shard_map/all_to_all | solution.py:50
  452.6 23.0 %collective-permute-start.7 = (bf16[256,128]{0,1:T(8,128)(2,1)}, bf16[256,128]{0,1:T(8,128)(2,1)}, u32[]{:S(2)}, u32[]{:S(2)}) collective-permute-start(bf16[256,128]{0,1:T(8,128)(2,1)} %get-tuple-element.21), channel_id=1, source_target_pairs={{16,0},{24,8},{32,16},{40,24},{48,32},{56,40},{64,48},{72,56},{80,... | collective-permute-start | bytes 196616 | tf_op jit(solution)/shard_map/ppermute | solution.py:40
  460.3 15.3 %collective-permute-start.6 = (bf16[256,128]{0,1:T(8,128)(2,1)}, bf16[256,128]{0,1:T(8,128)(2,1)}, u32[]{:S(2)}, u32[]{:S(2)}) collective-permute-start(bf16[256,128]{0,1:T(8,128)(2,1)} %get-tuple-element.20), channel_id=1, source_target_pairs={{8,0},{16,8},{24,16},{32,24},{40,32},{48,40},{56,48},{64,56},{72,6... | collective-permute-start | bytes 196616 | tf_op jit(solution)/shard_map/ppermute | solution.py:40
  462.4 4.5 copy-start.5
  470.2 10.2 %collective-permute-start.5 = (bf16[256,128]{1,0:T(8,128)(2,1)}, bf16[256,128]{1,0:T(8,128)(2,1)S(1)}, u32[]{:S(2)}, u32[]{:S(2)}) collective-permute-start(bf16[256,128]{1,0:T(8,128)(2,1)} %get-tuple-element.23), channel_id=1, source_target_pairs={{16,0},{24,8},{32,16},{40,24},{48,32},{56,40},{64,48},{72,56},{80,... | collective-permute-start | bytes 196616 | tf_op jit(solution)/shard_map/ppermute | solution.py:40
  472.3 9.7 %collective-permute-start.4 = (bf16[256,128]{1,0:T(8,128)(2,1)}, bf16[256,128]{1,0:T(8,128)(2,1)S(1)}, u32[]{:S(2)}, u32[]{:S(2)}) collective-permute-start(bf16[256,128]{1,0:T(8,128)(2,1)} %get-tuple-element.22), channel_id=1, source_target_pairs={{8,0},{16,8},{24,16},{32,24},{40,32},{48,40},{56,48},{64,56},{72,6... | collective-permute-start | bytes 196616 | tf_op jit(solution)/shard_map/ppermute | solution.py:40
